TPU v7x, 32 devices: a whole 2x2x4 slice. The times are simulated.
32 devices in a mesh: dom: 8 (over z, x), dir: 4 (over y, core).
Axes of the slice: x: 2, y: 2, z: 4, core: 2. Of those that a mesh axis runs over, the one named last changes fastest.
Arguments:
- x_edges: bfloat16 [65536, 128], P(('dom', 'dir')), may hold values from -6 to 6
- send_list: int32 [1024, 32], P(('dom', 'dir')), may hold values from 0 to 2048, as said below
- connectivity: int32 [6, 32768], P(None, ('dom', 'dir')), may hold values from 0 to 3071, as said below
- elem_mats: float32 [36, 32768], P(None, ('dom', 'dir'))
- elem_live: int32 [32], P(('dom', 'dir')), may hold values from 512 to 1024, as said below
- currents: bfloat16 [1024, 128, 128], P(('dom', 'dir')), may hold values from -0.1796875 to 0.1796875
- positions: bfloat16 [1024, 3, 128], P(('dom', 'dir')), may hold values from -1 to 1
- block_live: int32 [1024], P(('dom', 'dir')), may hold values from 32 to 128
- block_owner: int32 [1024], P(('dom', 'dir')), may hold values from 0 to 7, as said below
- block_leaf: int32 [1024], P(('dom', 'dir')), may hold values from 0 to 15
- cone_waves: float32 [3, 16], P(None, 'dir'), may hold values from -6 to 6
Outputs:
- interior_out: float32 [65536, 128], P(('dom', 'dir'))
- expansions: float32 [16, 16, 2, 64, 128], P('dom', 'dir')
Inputs may be any that keep to these rules, and one draw needn't show every extreme that they name: `send_list`: in row a * 32 + b the used entries come first and name owned edges of a; the rest are 2048. A partition reads nothing of itself; some pair uses all 32 entries. `connectivity`: entries below 2048 are owned edges; 2048 + p * 32 + s names the s-th edge that partition p lists for this partition, and only used entries are named. `elem_live`: elements at positions from this count on are padding; some partition has all 1024. `block_owner`: among the 32 blocks of one partition at most 12 name one leaf owner; some leaf owner is named by exactly 12 blocks of every partition.
All inputs are finite; a program needn't handle non-finite values.
Results may differ from a plain program's by a relative error of at most 0.0056.
Values may be sent and summed in bfloat16 or wider, within the bound.
A program may use at most 128 MiB of HBM per device.

v0:
```python
import jax
import jax.numpy as jnp
from jax import lax
from jax.sharding import PartitionSpec as P

LEAVES_DEV = 16
NODES = 4


def cheb_points():
    node_order = jnp.arange(NODES).astype(jnp.float32)
    return jnp.cos((2.0 * node_order + 1.0) * (jnp.pi / (2.0 * NODES)))


def lagrange(points):
    node_values = cheb_points()
    rows_out = []
    for target in range(NODES):
        product = jnp.ones_like(points)
        for other_node in range(NODES):
            if other_node != target:
                product = (
                    product
                    * (points - node_values[other_node])
                    / (node_values[target] - node_values[other_node])
                )
        rows_out.append(product)
    return jnp.stack(rows_out, axis=-2)


def tensor_basis(coords):
    first = lagrange(coords[..., 0, :])
    second = lagrange(coords[..., 1, :])
    third = lagrange(coords[..., 2, :])
    joined = (
        first[..., :, None, None, :] * second[..., None, :, None, :] * third[..., None, None, :, :]
    )
    return joined.reshape(coords.shape[:-2] + (NODES**3, coords.shape[-1]))


def node_coords():
    ladder = jnp.arange(NODES**3)
    digits = jnp.stack([ladder // (NODES * NODES), ladder // NODES % NODES, ladder % NODES]).astype(
        jnp.float32
    )
    return jnp.cos((2.0 * digits + 1.0) * (jnp.pi / (2.0 * NODES)))


def wave_phase(waves, coords):
    return (
        waves[0][:, None] * coords[..., None, 0, :]
        + waves[1][:, None] * coords[..., None, 1, :]
        + waves[2][:, None] * coords[..., None, 2, :]
    )


def m2m_tables(waves):
    octant = jnp.arange(8)
    shifts = jnp.stack([octant // 4, octant // 2 % 2, octant % 2], axis=1).astype(jnp.float32) - 0.5
    points = shifts[:, :, None] + 0.5 * cheb_points()[None, None, :]
    weights = lagrange(points)
    first = weights[:, 0]
    second = weights[:, 1]
    third = weights[:, 2]
    joined = (
        first[:, :, None, None, :, None, None]
        * second[:, None, :, None, None, :, None]
        * third[:, None, None, :, None, None, :]
    )
    square = NODES**3
    joined = joined.reshape(8, square, square)
    child = shifts[:, :, None] + 0.5 * node_coords()[None]
    spread = child[:, :, None, :] - node_coords()[None, :, :, None]
    psi = 2.0 * (
        waves[0][:, None, None, None] * spread[None, :, 0]
        + waves[1][:, None, None, None] * spread[None, :, 1]
        + waves[2][:, None, None, None] * spread[None, :, 2]
    )
    table_real = (joined[None] * jnp.cos(psi)).astype(jnp.bfloat16)
    table_imag = (-joined[None] * jnp.sin(psi)).astype(jnp.bfloat16)
    return (table_real, table_imag)


def pack_slots(owners, dest_count, capacity, members):
    matches = (owners[:, None] == jnp.arange(dest_count)[None, :]).astype(jnp.int32)
    ranking = jnp.sum((jnp.cumsum(matches, axis=0) - matches) * matches, axis=1)
    slot_index = owners * capacity + ranking
    source_row = (
        jnp.full((dest_count * capacity,), owners.shape[0], jnp.int32)
        .at[slot_index]
        .set(jnp.arange(owners.shape[0], dtype=jnp.int32))
    )
    padded = [
        jnp.concatenate([member, jnp.zeros((1,) + member.shape[1:], member.dtype)])
        for member in members
    ]
    return tuple((array_now[source_row] for array_now in padded))


def interior_part(x_edges, send_list, connectivity, elem_mats, elem_live):
    owned_rows, columns = x_edges.shape
    partitions, slot_width = send_list.shape
    element_count = connectivity.shape[1]
    padded = jnp.concatenate([x_edges, jnp.zeros((1, columns), x_edges.dtype)])
    outgoing = padded[send_list]
    received = lax.all_to_all(outgoing, ("dom", "dir"), split_axis=0, concat_axis=0, tiled=True)
    edge_table = jnp.concatenate([x_edges, received.reshape(partitions * slot_width, columns)])
    gathered = edge_table[connectivity]
    live_mask = (jnp.arange(element_count) < elem_live[0])[:, None]
    term_list = []
    for row_index in range(6):
        summed = jnp.zeros((element_count, columns), jnp.float32)
        for col_index in range(6):
            summed = summed + elem_mats[row_index * 6 + col_index][:, None] * gathered[col_index]
        term_list.append(jnp.where(live_mask, summed, jnp.zeros_like(summed)))
    stacked = jnp.stack(term_list).reshape(6 * element_count, columns)
    assembled = jax.ops.segment_sum(
        stacked, connectivity.reshape(-1), num_segments=owned_rows + partitions * slot_width
    )
    back_terms = assembled[owned_rows:]
    returned = lax.all_to_all(
        back_terms.reshape(partitions, slot_width, columns),
        ("dom", "dir"),
        split_axis=0,
        concat_axis=0,
        tiled=True,
    )
    folded = jax.ops.segment_sum(
        returned.reshape(-1, columns), send_list.reshape(-1), num_segments=owned_rows + 1
    )
    return assembled[:owned_rows] + folded[:owned_rows]


def expand_leaves(arrived_blocks, arrived_meta, waves):
    block_size = arrived_blocks.shape[1]
    columns = arrived_blocks.shape[2]
    cone_count = waves.shape[1]
    square = NODES**3
    group_rows = 512 // cone_count
    group_count = arrived_blocks.shape[0] // group_rows
    leaf_ids = arrived_meta[:, 3, 0].astype(jnp.int32)

    def one_group(carry, inputs):
        real_sum, imag_sum = carry
        blocks_now, coords, leaves = inputs
        coords_wide = coords.astype(jnp.float32)
        basis_now = tensor_basis(coords_wide)
        phase_now = wave_phase(waves, coords_wide)
        real_w = (basis_now[:, None] * jnp.cos(phase_now)[:, :, None, :]).astype(jnp.bfloat16)
        imag_w = (-basis_now[:, None] * jnp.sin(phase_now)[:, :, None, :]).astype(jnp.bfloat16)
        real_part = jnp.einsum(
            "gcqb,gbn->gcqn", real_w, blocks_now, preferred_element_type=jnp.float32
        ).astype(jnp.bfloat16)
        imag_part = jnp.einsum(
            "gcqb,gbn->gcqn", imag_w, blocks_now, preferred_element_type=jnp.float32
        ).astype(jnp.bfloat16)
        selector = (jnp.arange(LEAVES_DEV)[:, None] == leaves[None, :]).astype(jnp.bfloat16)
        real_sum = real_sum + jnp.einsum(
            "lg,gcqn->lcqn", selector, real_part, preferred_element_type=jnp.float32
        )
        imag_sum = imag_sum + jnp.einsum(
            "lg,gcqn->lcqn", selector, imag_part, preferred_element_type=jnp.float32
        )
        return ((real_sum, imag_sum), None)

    empty = jnp.zeros((LEAVES_DEV, cone_count, square, columns), jnp.float32)
    inputs = (
        arrived_blocks.reshape(group_count, group_rows, block_size, columns),
        arrived_meta[:, :3].reshape(group_count, group_rows, 3, block_size),
        leaf_ids.reshape(group_count, group_rows),
    )
    sums, unused = lax.scan(one_group, (empty, empty), inputs)
    real_sum, imag_sum = sums
    node_phase = wave_phase(waves, node_coords())
    cosine = jnp.cos(node_phase)[None, :, :, None]
    sine_part = jnp.sin(node_phase)[None, :, :, None]
    leaf_real = (cosine * real_sum - sine_part * imag_sum).astype(jnp.bfloat16)
    leaf_imag = (cosine * imag_sum + sine_part * real_sum).astype(jnp.bfloat16)
    table_real, table_imag = m2m_tables(waves)
    child_real = leaf_real.reshape(LEAVES_DEV // 8, 8, cone_count, square, columns)
    child_imag = leaf_imag.reshape(LEAVES_DEV // 8, 8, cone_count, square, columns)
    parent_real = jnp.einsum(
        "cops,xocsn->xcpn", table_real, child_real, preferred_element_type=jnp.float32
    ) - jnp.einsum("cops,xocsn->xcpn", table_imag, child_imag, preferred_element_type=jnp.float32)
    parent_imag = jnp.einsum(
        "cops,xocsn->xcpn", table_real, child_imag, preferred_element_type=jnp.float32
    ) + jnp.einsum("cops,xocsn->xcpn", table_imag, child_real, preferred_element_type=jnp.float32)
    return jnp.stack([parent_real, parent_imag], axis=2)


def boundary_part(currents, positions, block_live, block_owner, block_leaf, cone_waves):
    block_count, block_size, columns = currents.shape
    dom_count = lax.axis_size("dom")
    capacity = 3 * block_count // dom_count
    live_mask = jnp.arange(block_size)[None, :] < block_live[:, None]
    masked = jnp.where(live_mask[:, :, None], currents, jnp.zeros_like(currents))
    leaf_row = jnp.broadcast_to(
        block_leaf.astype(jnp.bfloat16)[:, None, None], (block_count, 1, block_size)
    )
    described = jnp.concatenate([positions, leaf_row], axis=1)
    packed_blocks, packed_meta = pack_slots(block_owner, dom_count, capacity, (masked, described))
    owner_blocks, owner_meta = (
        lax.all_to_all(packed_blocks, "dom", split_axis=0, concat_axis=0, tiled=True),
        lax.all_to_all(packed_meta, "dom", split_axis=0, concat_axis=0, tiled=True),
    )
    arrived_blocks, arrived_meta = (
        lax.all_gather(owner_blocks, "dir", axis=0, tiled=True),
        lax.all_gather(owner_meta, "dir", axis=0, tiled=True),
    )
    parents = expand_leaves(arrived_blocks, arrived_meta, cone_waves)
    return parents


def shards(
    x_edges,
    send_list,
    connectivity,
    elem_mats,
    elem_live,
    currents,
    positions,
    block_live,
    block_owner,
    block_leaf,
    cone_waves,
):
    interior_out = interior_part(x_edges, send_list, connectivity, elem_mats, elem_live)
    expansions = boundary_part(currents, positions, block_live, block_owner, block_leaf, cone_waves)
    return (interior_out, expansions)


def solution(mesh):
    placed = (
        P(("dom", "dir"), None),
        P(("dom", "dir"), None),
        P(None, ("dom", "dir")),
        P(None, ("dom", "dir")),
        P(("dom", "dir")),
        P(("dom", "dir"), None, None),
        P(("dom", "dir"), None, None),
        P(("dom", "dir")),
        P(("dom", "dir")),
        P(("dom", "dir")),
        P(None, "dir"),
    )
    return jax.shard_map(
        shards,
        mesh=mesh,
        in_specs=placed,
        out_specs=(P(("dom", "dir"), None), P("dom", "dir", None, None, None)),
        check_vma=False,
    )
```

profile of v0, /device:TPU:1, one launch (start us, length us, event | category | flops | bytes accessed | tf_op | source)
XLA Modules:
  0.0 447.2 jit_solution(9750463956113787339)
XLA Ops:
  13.6 2.7 gather_fusion.3
  16.3 76.3 %all_to_all.20 = bf16[96,128,128]{2,1,0:T(8,128)(2,1)} all-to-all(bf16[96,128,128]{2,1,0:T(8,128)(2,1)} %gather_fusion.3), channel_id=1, replica_groups=mesh['dom'=8,'dir'=4] {'dom'}, dimensions={0} | all-to-all | bytes 6291456 | tf_op jit(solution)/shard_map/all_to_all | solution.py:203
  93.6 4.3 gather_fusion
  97.9 5.2 %all-to-all-start = ((bf16[32,32,128]{2,1,0:T(8,128)(2,1)}), bf16[32,32,128]{2,1,0:T(8,128)(2,1)S(1)}, u32[]{:S(2)}, u32[]{:S(2)}) async-start(bf16[32,32,128]{2,1,0:T(8,128)(2,1)} %bitcast.2), calls=%async_computation | async-start | bytes 524288 | tf_op jit(solution)/shard_map/all_to_all | solution.py:106
  119.4 2.5 fusion.102
  127.2 1.8 copy.37
  130.4 3.3 copy.39
  134.5 5.7 %all-to-all-start.2 = ((bf16[96,4,128]{2,1,0:T(4,128)(2,1)}), bf16[96,4,128]{2,1,0:T(4,128)(2,1)S(1)}, u32[]{:S(2)}, u32[]{:S(2)}) async-start(bf16[96,4,128]{2,1,0:T(4,128)(2,1)} %gather_fusion.2), calls=%async_computation.2 | async-start | bytes 196608 | tf_op jit(solution)/shard_map/all_to_all | solution.py:204
  140.3 18.1 %gather_fusion.1 = bf16[6144,128]{1,0:T(8,128)(2,1)S(1)} fusion(bf16[3072,128]{1,0:T(8,128)(2,1)S(1)} %pad_maximum_fusion.3, s32[6144]{0:T(1024)S(1)} %broadcast_clamp_fusion), kind=kCustom, calls=%fused_computation.1 | custom fusion | bytes 3170304 | tf_op jit(solution)/shard_map/gather | solution.py:108
  168.0 33.9 %scatter_custom_fusion = f32[3072,128]{1,0:T(8,128)S(1)} fusion(s32[6144]{0:T(1024)} %reshape.1056, f32[6144,128]{1,0:T(8,128)} %bitcast.296, f32[]{:T(128)} %constant.151.clone.1), kind=kCustom, calls=%fused_computation.118 | custom fusion | flops 786432 | bytes 1573376 | tf_op jit(solution)/shard_map/scatter-add | solution.py:117
  202.8 6.4 %all-to-all-start.1 = ((f32[32,32,128]{2,1,0:T(8,128)}), f32[32,32,128]{2,1,0:T(8,128)S(1)}, u32[]{:S(2)}, u32[]{:S(2)}) async-start(f32[32,32,128]{2,1,0:T(8,128)} %bitcast.52), calls=%async_computation.1 | async-start | bytes 1048576 | tf_op jit(solution)/shard_map/all_to_all | solution.py:121
  210.6 9.4 %all_gather.6 = bf16[384,4,128]{2,1,0:T(4,128)(2,1)S(1)} all-gather(bf16[96,4,128]{2,1,0:T(4,128)(2,1)S(1)} %all-to-all-done.2), channel_id=1, replica_groups=mesh['dom'=8,'dir'=4] {'dir'}, dimensions={0}, use_global_device_ids=true | all-gather | bytes 491520 | tf_op jit(solution)/shard_map/all_gather | solution.py:208
  220.1 6.9 %fusion.84 = s32[384]{0:T(512)S(1)} fusion(bf16[384,4,128]{2,1,0:T(4,128)(2,1)S(1)} %all_gather.6), kind=kLoop, calls=%fused_computation.178 | loop fusion | flops 384 | bytes 2304 | tf_op jit(solution)/shard_map/convert_element_type | solution.py:141
  227.8 7.3 %scatter_custom_fusion.1 = f32[2049,128]{1,0:T(8,128)S(1)} fusion(s32[1024]{0:T(1024)} %reshape.1064, f32[1024,128]{1,0:T(8,128)} %bitcast.295, f32[]{:T(128)} %constant.151.clone.1), kind=kCustom, calls=%fused_computation.120 | custom fusion | flops 131072 | bytes 1049600 | tf_op jit(solution)/shard_map/scatter-add | solution.py:128
  235.0 2.3 slice_add_fusion
  237.3 183.9 %while.13 = (s32[]{:T(128)}, f32[16,4,64,128]{3,0,2,1:T(8,128)S(1)}, f32[16,4,64,128]{3,0,2,1:T(8,128)}, s32[3,128]{1,0:T(4,128)S(1)}, bf16[3,128,3,128]{3,1,2,0...) while((s32[]{:T(128)}, ...), condition=%wide.region_6.7_spmd.clone, body=%wide.region_5.6_spmd.clone.sunk | while | flops 2447904768 | bytes 113871504 | solution.py:172
  260.6 2.6 multiply_divide_fusion.15
  267.0 2.6 multiply_divide_fusion.16
  269.6 2.1 fusion.150
  271.7 2.6 multiply_divide_fusion.17
  276.5 2.0 copy-done
  278.5 6.9 %fusion.151 = bf16[128,4,64,128]{3,2,1,0:T(8,128)(2,1)} fusion(f32[128,4,128]{2,1,0:T(4,128)S(1)} %get-tuple-element.266, f32[128,64,128]{2,1,0:T(8,128)S(1)} %bitcast.288, bf16[3,128,128,128]{3,2,1,0:T(8,128)(2,1)} %get-tuple-element.306, s32[]{:T(128)S(6)} %copy.78), kind=kOutput, calls=%fused_computation.20.clone.1 | convolution fusion | flops 1086324736 | bytes 17039364 | tf_op jit(solution)/shard_map/while/body/eval_jaxpr/gcqb,gbn->gcqn/dot_general | solution.py:151
  285.5 8.2 %select_add_fusion.4 = f32[16,4,64,128]{3,0,2,1:T(8,128)S(1)} fusion(f32[16,4,64,128]{3,0,2,1:T(8,128)S(1)} %get-tuple-element.292, bf16[128,4,64,128]{3,2,1,0:T(8,128)(2,1)} %fusion.151, pred[]{:T(512)S(6)} %compare.55, s32[128]{0:T(128)S(1)} %fusion.152), kind=kOutput, calls=%fused_computation.26.clone.1 | convolution fusion | flops 135268352 | bytes 12583425 | tf_op jit(solution)/shard_map/while/body/eval_jaxpr/lg,gcqn->lcqn/dot_general | solution.py:158
  294.1 4.8 %fusion.153 = bf16[128,4,64,128]{3,2,1,0:T(8,128)(2,1)S(1)} fusion(f32[128,4,128]{2,1,0:T(4,128)S(1)} %get-tuple-element.281, f32[128,64,128]{2,1,0:T(8,128)S(1)} %neg.19, bf16[3,128,128,128]{3,2,1,0:T(8,128)(2,1)} %get-tuple-element.306, s32[]{:T(128)S(6)} %copy.78), kind=kOutput, calls=%fused_computation.19.clone.1 | convolution fusion | flops 1086324736 | bytes 17039364 | tf_op jit(solution)/shard_map/while/body/eval_jaxpr/gcqb,gbn->gcqn/dot_general | solution.py:154
  299.0 6.0 %select_add_fusion.5 = f32[16,4,64,128]{3,0,2,1:T(8,128)} fusion(f32[16,4,64,128]{3,0,2,1:T(8,128)} %get-tuple-element.293, bf16[128,4,64,128]{3,2,1,0:T(8,128)(2,1)S(1)} %fusion.153, pred[]{:T(512)S(6)} %compare.55, s32[128]{0:T(128)S(1)} %fusion.152), kind=kOutput, calls=%fused_computation.25.clone.1 | convolution fusion | flops 135268352 | bytes 12583425 | tf_op jit(solution)/shard_map/while/body/eval_jaxpr/lg,gcqn->lcqn/dot_general | solution.py:161
  317.0 2.6 multiply_divide_fusion.15
  323.4 2.6 multiply_divide_fusion.16
  326.0 2.1 fusion.150
  328.1 2.6 multiply_divide_fusion.17
  332.9 2.0 copy-done
  335.0 6.9 %fusion.151 = bf16[128,4,64,128]{3,2,1,0:T(8,128)(2,1)} fusion(f32[128,4,128]{2,1,0:T(4,128)S(1)} %get-tuple-element.266, f32[128,64,128]{2,1,0:T(8,128)S(1)} %bitcast.288, bf16[3,128,128,128]{3,2,1,0:T(8,128)(2,1)} %get-tuple-element.306, s32[]{:T(128)S(6)} %copy.78), kind=kOutput, calls=%fused_computation.20.clone.1 | convolution fusion | flops 1086324736 | bytes 17039364 | tf_op jit(solution)/shard_map/while/body/eval_jaxpr/gcqb,gbn->gcqn/dot_general | solution.py:151
  341.9 8.2 %select_add_fusion.4 = f32[16,4,64,128]{3,0,2,1:T(8,128)S(1)} fusion(f32[16,4,64,128]{3,0,2,1:T(8,128)S(1)} %get-tuple-element.292, bf16[128,4,64,128]{3,2,1,0:T(8,128)(2,1)} %fusion.151, pred[]{:T(512)S(6)} %compare.55, s32[128]{0:T(128)S(1)} %fusion.152), kind=kOutput, calls=%fused_computation.26.clone.1 | convolution fusion | flops 135268352 | bytes 12583425 | tf_op jit(solution)/shard_map/while/body/eval_jaxpr/lg,gcqn->lcqn/dot_general | solution.py:158
  350.6 4.8 %fusion.153 = bf16[128,4,64,128]{3,2,1,0:T(8,128)(2,1)S(1)} fusion(f32[128,4,128]{2,1,0:T(4,128)S(1)} %get-tuple-element.281, f32[128,64,128]{2,1,0:T(8,128)S(1)} %neg.19, bf16[3,128,128,128]{3,2,1,0:T(8,128)(2,1)} %get-tuple-element.306, s32[]{:T(128)S(6)} %copy.78), kind=kOutput, calls=%fused_computation.19.clone.1 | convolution fusion | flops 1086324736 | bytes 17039364 | tf_op jit(solution)/shard_map/while/body/eval_jaxpr/gcqb,gbn->gcqn/dot_general | solution.py:154
  355.4 7.6 %select_add_fusion.5 = f32[16,4,64,128]{3,0,2,1:T(8,128)} fusion(f32[16,4,64,128]{3,0,2,1:T(8,128)} %get-tuple-element.293, bf16[128,4,64,128]{3,2,1,0:T(8,128)(2,1)S(1)} %fusion.153, pred[]{:T(512)S(6)} %compare.55, s32[128]{0:T(128)S(1)} %fusion.152), kind=kOutput, calls=%fused_computation.25.clone.1 | convolution fusion | flops 135268352 | bytes 12583425 | tf_op jit(solution)/shard_map/while/body/eval_jaxpr/lg,gcqn->lcqn/dot_general | solution.py:161
  375.1 2.6 multiply_divide_fusion.15
  381.5 2.6 multiply_divide_fusion.16
  384.1 2.1 fusion.150
  386.1 2.6 multiply_divide_fusion.17
  391.0 2.0 copy-done
  393.0 6.9 %fusion.151 = bf16[128,4,64,128]{3,2,1,0:T(8,128)(2,1)} fusion(f32[128,4,128]{2,1,0:T(4,128)S(1)} %get-tuple-element.266, f32[128,64,128]{2,1,0:T(8,128)S(1)} %bitcast.288, bf16[3,128,128,128]{3,2,1,0:T(8,128)(2,1)} %get-tuple-element.306, s32[]{:T(128)S(6)} %copy.78), kind=kOutput, calls=%fused_computation.20.clone.1 | convolution fusion | flops 1086324736 | bytes 17039364 | tf_op jit(solution)/shard_map/while/body/eval_jaxpr/gcqb,gbn->gcqn/dot_general | solution.py:151
  399.9 8.2 %select_add_fusion.4 = f32[16,4,64,128]{3,0,2,1:T(8,128)S(1)} fusion(f32[16,4,64,128]{3,0,2,1:T(8,128)S(1)} %get-tuple-element.292, bf16[128,4,64,128]{3,2,1,0:T(8,128)(2,1)} %fusion.151, pred[]{:T(512)S(6)} %compare.55, s32[128]{0:T(128)S(1)} %fusion.152), kind=kOutput, calls=%fused_computation.26.clone.1 | convolution fusion | flops 135268352 | bytes 12583425 | tf_op jit(solution)/shard_map/while/body/eval_jaxpr/lg,gcqn->lcqn/dot_general | solution.py:158
  408.6 4.8 %fusion.153 = bf16[128,4,64,128]{3,2,1,0:T(8,128)(2,1)S(1)} fusion(f32[128,4,128]{2,1,0:T(4,128)S(1)} %get-tuple-element.281, f32[128,64,128]{2,1,0:T(8,128)S(1)} %neg.19, bf16[3,128,128,128]{3,2,1,0:T(8,128)(2,1)} %get-tuple-element.306, s32[]{:T(128)S(6)} %copy.78), kind=kOutput, calls=%fused_computation.19.clone.1 | convolution fusion | flops 1086324736 | bytes 17039364 | tf_op jit(solution)/shard_map/while/body/eval_jaxpr/gcqb,gbn->gcqn/dot_general | solution.py:154
  413.4 7.6 %select_add_fusion.5 = f32[16,4,64,128]{3,0,2,1:T(8,128)} fusion(f32[16,4,64,128]{3,0,2,1:T(8,128)} %get-tuple-element.293, bf16[128,4,64,128]{3,2,1,0:T(8,128)(2,1)S(1)} %fusion.153, pred[]{:T(512)S(6)} %compare.55, s32[128]{0:T(128)S(1)} %fusion.152), kind=kOutput, calls=%fused_computation.25.clone.1 | convolution fusion | flops 135268352 | bytes 12583425 | tf_op jit(solution)/shard_map/while/body/eval_jaxpr/lg,gcqn->lcqn/dot_general | solution.py:161
  421.3 2.1 fusion.35
  423.5 3.8 convolution_bitcast_fusion
  427.3 3.8 convolution_bitcast_fusion.2
  431.1 3.8 fusion.33
  435.0 4.1 fusion.31
  (226 shorter events, 39.1 us)
Async XLA Ops:
  7.2 230.2 %all-gather.2.cloned.1.call-start = ((), (), s32[]{:S(2)}) async-start(), calls=%async_computation.4 | async-start | bytes 15728640 | tf_op jit(solution)/shard_map/all_gather | solution.py:207
  92.5 26.6 %copy-start.12 = (s32[6,1024]{1,0:T(8,128)S(1)}, s32[6,1024]{1,0:T(8,128)}, u32[]{:S(2)}) copy-start(s32[6,1024]{1,0:T(8,128)} %param.15) | copy-start | bytes 73732
  92.5 26.6 %copy-start.57 = (s32[32]{0:T(128)S(1)}, s32[32]{0:T(128)}, u32[]{:S(2)}) copy-start(s32[32]{0:T(128)} %param.22) | copy-start | bytes 388
  92.5 26.6 %copy-start.16 = (bf16[32,3,128]{2,0,1:T(8,128)(2,1)S(1)}, bf16[32,3,128]{2,0,1:T(8,128)(2,1)}, u32[]{:S(2)}) copy-start(bf16[32,3,128]{2,0,1:T(8,128)(2,1)} %param.19) | copy-start | bytes 73732
  92.5 30.1 %copy-start.15 = (f32[3,4]{1,0:T(4,128)S(1)}, f32[3,4]{1,0:T(4,128)}, u32[]{:S(2)}) copy-start(f32[3,4]{1,0:T(4,128)} %param.23) | copy-start | bytes 148
  92.5 30.7 %copy-start.11 = (f32[36,1024]{1,0:T(8,128)S(1)}, f32[36,1024]{1,0:T(8,128)}, u32[]{:S(2)}) copy-start(f32[36,1024]{1,0:T(8,128)} %param.16) | copy-start | bytes 442372
  93.6 30.9 %copy-start.14 = (s32[32,32]{1,0:T(8,128)S(1)}, s32[32,32]{1,0:T(8,128)}, u32[]{:S(2)}) copy-start(s32[32,32]{1,0:T(8,128)} %param.14) | copy-start | bytes 12292
  97.9 36.6 %all-to-all-start = ((bf16[32,32,128]{2,1,0:T(8,128)(2,1)}), bf16[32,32,128]{2,1,0:T(8,128)(2,1)S(1)}, u32[]{:S(2)}, u32[]{:S(2)}) async-start(bf16[32,32,128]{2,1,0:T(8,128)(2,1)} %bitcast.2), calls=%async_computation | async-start | bytes 524288 | tf_op jit(solution)/shard_map/all_to_all | solution.py:106
  119.3 7.9 %copy-start.49 = (f32[3,64]{1,0:T(4,128)}, f32[3,64]{1,0:T(4,128)S(1)}, u32[]{:S(2)}) copy-start(f32[3,64]{1,0:T(4,128)S(1)} %get-tuple-element.176) | copy-start | bytes 2308
  134.5 68.3 %all-to-all-start.2 = ((bf16[96,4,128]{2,1,0:T(4,128)(2,1)}), bf16[96,4,128]{2,1,0:T(4,128)(2,1)S(1)}, u32[]{:S(2)}, u32[]{:S(2)}) async-start(bf16[96,4,128]{2,1,0:T(4,128)(2,1)} %gather_fusion.2), calls=%async_computation.2 | async-start | bytes 196608 | tf_op jit(solution)/shard_map/all_to_all | solution.py:204
  140.2 18.3 %copy-start.24 = (f32[1,1024]{1,0:T(1,128)S(1)}, f32[1,1024]{1,0:T(1,128)}, u32[]{:S(2)}) copy-start(f32[1,1024]{1,0:T(1,128)} %get-tuple-element.153) | copy-start | bytes 12292
  140.2 18.3 %copy-start.25 = (f32[1,1024]{1,0:T(1,128)S(1)}, f32[1,1024]{1,0:T(1,128)}, u32[]{:S(2)}) copy-start(f32[1,1024]{1,0:T(1,128)} %get-tuple-element.154) | copy-start | bytes 12292
  140.2 18.3 %copy-start.26 = (f32[1,1024]{1,0:T(1,128)S(1)}, f32[1,1024]{1,0:T(1,128)}, u32[]{:S(2)}) copy-start(f32[1,1024]{1,0:T(1,128)} %get-tuple-element.155) | copy-start | bytes 12292
  140.2 18.3 %copy-start.27 = (f32[1,1024]{1,0:T(1,128)S(1)}, f32[1,1024]{1,0:T(1,128)}, u32[]{:S(2)}) copy-start(f32[1,1024]{1,0:T(1,128)} %get-tuple-element.156) | copy-start | bytes 12292
  140.3 18.3 %copy-start.28 = (f32[1,1024]{1,0:T(1,128)S(1)}, f32[1,1024]{1,0:T(1,128)}, u32[]{:S(2)}) copy-start(f32[1,1024]{1,0:T(1,128)} %get-tuple-element.157) | copy-start | bytes 12292
  140.3 18.3 %copy-start.29 = (f32[1,1024]{1,0:T(1,128)S(1)}, f32[1,1024]{1,0:T(1,128)}, u32[]{:S(2)}) copy-start(f32[1,1024]{1,0:T(1,128)} %get-tuple-element.158) | copy-start | bytes 12292
  140.3 19.5 %copy-start.18 = (f32[1,1024]{1,0:T(1,128)S(1)}, f32[1,1024]{1,0:T(1,128)}, u32[]{:S(2)}) copy-start(f32[1,1024]{1,0:T(1,128)} %get-tuple-element.147) | copy-start | bytes 12292
  140.3 19.5 %copy-start.19 = (f32[1,1024]{1,0:T(1,128)S(1)}, f32[1,1024]{1,0:T(1,128)}, u32[]{:S(2)}) copy-start(f32[1,1024]{1,0:T(1,128)} %get-tuple-element.148) | copy-start | bytes 12292
  140.3 19.5 %copy-start.20 = (f32[1,1024]{1,0:T(1,128)S(1)}, f32[1,1024]{1,0:T(1,128)}, u32[]{:S(2)}) copy-start(f32[1,1024]{1,0:T(1,128)} %get-tuple-element.149) | copy-start | bytes 12292
  140.3 19.5 %copy-start.21 = (f32[1,1024]{1,0:T(1,128)S(1)}, f32[1,1024]{1,0:T(1,128)}, u32[]{:S(2)}) copy-start(f32[1,1024]{1,0:T(1,128)} %get-tuple-element.150) | copy-start | bytes 12292
  140.3 19.5 %copy-start.22 = (f32[1,1024]{1,0:T(1,128)S(1)}, f32[1,1024]{1,0:T(1,128)}, u32[]{:S(2)}) copy-start(f32[1,1024]{1,0:T(1,128)} %get-tuple-element.151) | copy-start | bytes 12292
  140.3 19.5 %copy-start.23 = (f32[1,1024]{1,0:T(1,128)S(1)}, f32[1,1024]{1,0:T(1,128)}, u32[]{:S(2)}) copy-start(f32[1,1024]{1,0:T(1,128)} %get-tuple-element.152) | copy-start | bytes 12292
  158.5 3.9 copy-start.40
  158.5 3.9 copy-start.41
  158.5 3.9 copy-start.42
  158.6 3.9 copy-start.43
  158.6 3.9 copy-start.44
  158.6 3.9 copy-start.45
  159.9 3.9 copy-start.34
  159.9 3.9 copy-start.35
  161.2 3.9 copy-start.30
  161.2 3.9 copy-start.31
  161.2 3.9 copy-start.32
  161.2 3.9 copy-start.33
  165.0 44.2 %copy-start.51 = (f32[4]{0:T(128)S(1)}, f32[4]{0:T(128)}, u32[]{:S(2)}) copy-start(f32[4]{0:T(128)} %get-tuple-element.169) | copy-start | bytes 52
  165.0 44.2 %copy-start.52 = (f32[4]{0:T(128)S(1)}, f32[4]{0:T(128)}, u32[]{:S(2)}) copy-start(f32[4]{0:T(128)} %get-tuple-element.170) | copy-start | bytes 52
  165.0 44.2 %copy-start.53 = (f32[4]{0:T(128)S(1)}, f32[4]{0:T(128)}, u32[]{:S(2)}) copy-start(f32[4]{0:T(128)} %get-tuple-element.171) | copy-start | bytes 52
  165.0 44.2 %copy-start.54 = (f32[64]{0:T(128)S(1)}, f32[64]{0:T(128)}, u32[]{:S(2)}) copy-start(f32[64]{0:T(128)} %get-tuple-element.172) | copy-start | bytes 772
  165.1 44.2 %copy-start.55 = (f32[64]{0:T(128)S(1)}, f32[64]{0:T(128)}, u32[]{:S(2)}) copy-start(f32[64]{0:T(128)} %get-tuple-element.173) | copy-start | bytes 772
  165.1 44.2 %copy-start.56 = (f32[64]{0:T(128)S(1)}, f32[64]{0:T(128)}, u32[]{:S(2)}) copy-start(f32[64]{0:T(128)} %get-tuple-element.174) | copy-start | bytes 772
  165.1 44.3 %copy-start.50 = (f32[3,64]{1,0:T(4,128)S(1)}, f32[3,64]{1,0:T(4,128)}, u32[]{:S(2)}) copy-start(f32[3,64]{1,0:T(4,128)} %copy-done.49) | copy-start | bytes 2308
  201.9 7.8 %copy-start.3 = (f32[3072,128]{1,0:T(8,128)}, f32[3072,128]{1,0:T(8,128)S(1)}, u32[]{:S(2)}) copy-start(f32[3072,128]{1,0:T(8,128)S(1)} %scatter_custom_fusion) | copy-start | bytes 4718596
  202.8 24.1 %all-to-all-start.1 = ((f32[32,32,128]{2,1,0:T(8,128)}), f32[32,32,128]{2,1,0:T(8,128)S(1)}, u32[]{:S(2)}, u32[]{:S(2)}) async-start(f32[32,32,128]{2,1,0:T(8,128)} %bitcast.52), calls=%async_computation.1 | async-start | bytes 1048576 | tf_op jit(solution)/shard_map/all_to_all | solution.py:121
  210.6 26.7 %copy-start.2 = (f32[16,4,64,128]{3,0,2,1:T(8,128)S(1)}, f32[16,4,64,128]{3,0,2,1:T(8,128)}, u32[]{:S(2)}) copy-start(f32[16,4,64,128]{3,0,2,1:T(8,128)} %custom-call) | copy-start | bytes 6291460
  285.5 8.2 %copy-start.1 = (f32[128,4,4,4,128]{4,3,2,1,0:T(4,128)S(1)}, f32[128,4,4,4,128]{4,3,2,1,0:T(4,128)}, u32[]{:S(2)}) copy-start(f32[128,4,4,4,128]{4,3,2,1,0:T(4,128)} %copy-done) | copy-start | bytes 12582916 | tf_op jit(solution)/shard_map/while
  341.9 8.2 %copy-start.1 = (f32[128,4,4,4,128]{4,3,2,1,0:T(4,128)S(1)}, f32[128,4,4,4,128]{4,3,2,1,0:T(4,128)}, u32[]{:S(2)}) copy-start(f32[128,4,4,4,128]{4,3,2,1,0:T(4,128)} %copy-done) | copy-start | bytes 12582916 | tf_op jit(solution)/shard_map/while
  399.9 8.2 %copy-start.1 = (f32[128,4,4,4,128]{4,3,2,1,0:T(4,128)S(1)}, f32[128,4,4,4,128]{4,3,2,1,0:T(4,128)}, u32[]{:S(2)}) copy-start(f32[128,4,4,4,128]{4,3,2,1,0:T(4,128)} %copy-done) | copy-start | bytes 12582916 | tf_op jit(solution)/shard_map/while
  423.4 7.7 %copy-start.6 = (f32[8,64,64]{1,0,2:T(8,128)S(1)}, f32[8,64,64]{1,0,2:T(8,128)}, u32[]{:S(2)}) copy-start(f32[8,64,64]{1,0,2:T(8,128)} %copy.37) | copy-start | bytes 393220
  (18 other events, 44.6 us)
Sparse Core Ops, SparseCore 0:
  92.7 85.4 all-gather.1
where the time goes:
time: 454 us; the launch traced here: 447 us
  other arithmetic  107 us (24%)
  matrix products  96.7 us (21%)
  blocking collectives  85.7 us (19%)
  loops' own time  57 us (13%)
  local copies, waits for them, and re-layouts  53 us (12%)
  between operations  30.8 us (7%)
  starting transfers between devices  17.3 us (4%)
    all_to_all x1, blocking collectives, boundary_part(): lax.all_to_all(packed_blocks, 'dom', split_axis=0, concat_axis=0, tiled=T...  76.3 us
    another operation x1, loops' own time, expand_leaves(): sums, unused = lax.scan(one_group, (empty, empty), inputs)  57 us
    scatter-add x1, other arithmetic, interior_part(): jax.ops.segment_sum(stacked, connectivity.reshape(-1), num_segments=owned...  33.9 us
    div x10, other arithmetic, lagrange(): product * (points - node_values[other_node])  25.7 us
    dot_general x3, matrix products, one_group(): jnp.einsum('lg,gcqn->lcqn', selector, real_part, preferred_element_type=j...  24.6 us
    dot_general x3, matrix products, one_group(): jnp.einsum('lg,gcqn->lcqn', selector, imag_part, preferred_element_type=j...  21.3 us
    dot_general x3, matrix products, one_group(): jnp.einsum('gcqb,gbn->gcqn', real_w, blocks_now, preferred_element_type=j...  20.8 us
    gather x1, local copies, waits for them, and re-layouts, interior_part(): gathered = edge_table[connectivity]  18.1 us
  transfers between devices with their start and end apart: 4, of which 0 were waited for; matrix products, arithmetic and copies ran while one was open for 22% of the time, Pallas kernels for 0%

commit v1 on v0

--- a/solution.py
+++ b/solution.py
@@ -5,6 +5,29 @@
 
 LEAVES_DEV = 16
 NODES = 4
+
+
+def in_blocks(shard, dim, peers):
+    lengths = shard.shape
+    tiles = shard.reshape(*lengths[:dim], peers, lengths[dim] // peers, *lengths[dim + 1 :])
+    return jnp.moveaxis(tiles, dim, 0)
+
+
+def laid_out(tiles, dim):
+    dims = list(tiles.shape[1:])
+    dims[dim] *= tiles.shape[0]
+    return jnp.moveaxis(tiles, 0, dim).reshape(dims)
+
+
+def exchange_in_pairs(shard, axis, split_dim, concat_dim):
+    length, index = (lax.axis_size(axis), lax.axis_index(axis))
+    pieces = in_blocks(shard, split_dim, length)
+    outs = [pieces[index]]
+    for step in range(1, length):
+        sent = pieces[index ^ step]
+        outs.append(lax.ppermute(sent, axis, [(i, i ^ step) for i in range(length)]))
+    pieces = jnp.stack(outs)[index ^ jnp.arange(length)]
+    return laid_out(pieces, concat_dim)
 
 
 def cheb_points():
@@ -200,7 +223,7 @@
     described = jnp.concatenate([positions, leaf_row], axis=1)
     packed_blocks, packed_meta = pack_slots(block_owner, dom_count, capacity, (masked, described))
     owner_blocks, owner_meta = (
-        lax.all_to_all(packed_blocks, "dom", split_axis=0, concat_axis=0, tiled=True),
+        exchange_in_pairs(packed_blocks, "dom", 0, 0),
         lax.all_to_all(packed_meta, "dom", split_axis=0, concat_axis=0, tiled=True),
     )
     arrived_blocks, arrived_meta = (

time: 454 us -> 457 us (level)
  blocking collectives: 85.7 us -> 9.38 us
  waiting for transfers between devices: 0.03 us -> 44.8 us
  starting transfers between devices: 17.3 us -> 46.7 us
  local copies, waits for them, and re-layouts: 53 us -> 58.1 us
    all_to_all x1 -> x0, blocking collectives: 76.3 us -> none  [boundary_part(): lax.all_to_all(packed_blocks, 'dom', split_axis=0, concat_axis=0, tiled=T...]
    ppermute x0 -> x7, waiting for transfers between devices: none -> 44.7 us  [exchange_in_pairs(): lax.ppermute(sent, axis, [(i, i ^ step) for i in range(length)])]
    all_to_all x1, starting transfers between devices: 5.23 us -> 23.7 us  [interior_part(): lax.all_to_all(outgoing, ('dom', 'dir'), split_axis=0, concat_axis=0, til...]
    ppermute x0 -> x7, starting transfers between devices: none -> 10.9 us  [exchange_in_pairs(): lax.ppermute(sent, axis, [(i, i ^ step) for i in range(length)])]
  transfers between devices with their start and end apart: 4 -> 11, of which waited for: 0 -> 6; matrix products, arithmetic and copies ran while one was open for 22% -> 22% of each run, Pallas kernels for 0% -> 0%
where the time goes in v1:
time: 457 us; the launch traced here: 450 us
  other arithmetic  106 us (23%)
  matrix products  96.8 us (21%)
  local copies, waits for them, and re-layouts  58.1 us (13%)
  loops' own time  56.8 us (12%)
  starting transfers between devices  46.7 us (10%)
  waiting for transfers between devices  44.8 us (10%)
  between operations  30.8 us (7%)
  blocking collectives  9.38 us (2%)
    another operation x1, loops' own time, expand_leaves(): sums, unused = lax.scan(one_group, (empty, empty), inputs)  56.8 us
    ppermute x7, waiting for transfers between devices, exchange_in_pairs(): lax.ppermute(sent, axis, [(i, i ^ step) for i in range(length)])  44.7 us
    scatter-add x1, other arithmetic, interior_part(): jax.ops.segment_sum(stacked, connectivity.reshape(-1), num_segments=owned...  33.9 us
    div x10, other arithmetic, lagrange(): product * (points - node_values[other_node])  25.6 us
    dot_general x3, matrix products, one_group(): jnp.einsum('lg,gcqn->lcqn', selector, real_part, preferred_element_type=j...  24.6 us
    all_to_all x1, starting transfers between devices, interior_part(): lax.all_to_all(outgoing, ('dom', 'dir'), split_axis=0, concat_axis=0, til...  23.7 us
    dot_general x3, matrix products, one_group(): jnp.einsum('lg,gcqn->lcqn', selector, imag_part, preferred_element_type=j...  21.3 us
    dot_general x3, matrix products, one_group(): jnp.einsum('gcqb,gbn->gcqn', real_w, blocks_now, preferred_element_type=j...  20.9 us
  transfers between devices with their start and end apart: 11, of which 6 were waited for; matrix products, arithmetic and copies ran while one was open for 22% of the time, Pallas kernels for 0%

profile of v1, /device:TPU:1, one launch (start us, length us, event | category | flops | bytes accessed | tf_op | source)
XLA Modules:
  0.0 449.7 jit_solution(8631275246321632141)
XLA Ops:
  13.6 2.7 gather_fusion.3
  21.8 2.4 collective-permute-start.3
  25.2 4.1 collective-permute-done
  29.3 3.3 collective-permute-start.5
  32.7 13.5 %collective-permute-done.1 = bf16[12,128,128]{2,1,0:T(8,128)(2,1)S(1)} collective-permute-done((bf16[12,128,128]{2,1,0:T(8,128)(2,1)S(1)}, bf16[12,128,128]{2,1,0:T(8,128)(2,1)S(1)}, u32[]{:S(2)}, u32[]{:S(2)}) %collective-permute-start.1) | collective-permute-done | bytes 393248 | tf_op jit(solution)/shard_map/ppermute | solution.py:28
  46.9 7.1 %collective-permute-done.2 = bf16[12,128,128]{2,1,0:T(8,128)(2,1)S(1)} collective-permute-done((bf16[12,128,128]{2,1,0:T(8,128)(2,1)S(1)}, bf16[12,128,128]{2,1,0:T(8,128)(2,1)S(1)}, u32[]{:S(2)}, u32[]{:S(2)}) %collective-permute-start.2) | collective-permute-done | bytes 393248 | tf_op jit(solution)/shard_map/ppermute | solution.py:28
  54.7 11.3 %collective-permute-done.5 = bf16[12,128,128]{2,1,0:T(8,128)(2,1)S(1)} collective-permute-done((bf16[12,128,128]{2,1,0:T(8,128)(2,1)S(1)}, bf16[12,128,128]{2,1,0:T(8,128)(2,1)S(1)}, u32[]{:S(2)}, u32[]{:S(2)}) %collective-permute-start.5) | collective-permute-done | bytes 393248 | tf_op jit(solution)/shard_map/ppermute | solution.py:28
  66.0 8.3 %collective-permute-done.6 = bf16[12,128,128]{2,1,0:T(8,128)(2,1)S(1)} collective-permute-done((bf16[12,128,128]{2,1,0:T(8,128)(2,1)S(1)}, bf16[12,128,128]{2,1,0:T(8,128)(2,1)S(1)}, u32[]{:S(2)}, u32[]{:S(2)}) %collective-permute-start.6) | collective-permute-done | bytes 393248 | tf_op jit(solution)/shard_map/ppermute | solution.py:28
  74.4 2.6 gather_fusion.4
  78.1 4.3 gather_fusion
  82.4 23.7 %all-to-all-start = ((bf16[32,32,128]{2,1,0:T(8,128)(2,1)}), bf16[32,32,128]{2,1,0:T(8,128)(2,1)S(1)}, u32[]{:S(2)}, u32[]{:S(2)}) async-start(bf16[32,32,128]{2,1,0:T(8,128)(2,1)} %bitcast.2), calls=%async_computation | async-start | bytes 524288 | tf_op jit(solution)/shard_map/all_to_all | solution.py:129
  122.2 2.5 fusion.102
  133.2 3.3 copy.39
  137.3 5.7 %all-to-all-start.2 = ((bf16[96,4,128]{2,1,0:T(4,128)(2,1)}), bf16[96,4,128]{2,1,0:T(4,128)(2,1)S(1)}, u32[]{:S(2)}, u32[]{:S(2)}) async-start(bf16[96,4,128]{2,1,0:T(4,128)(2,1)} %gather_fusion.2), calls=%async_computation.2 | async-start | bytes 196608 | tf_op jit(solution)/shard_map/all_to_all | solution.py:227
  143.2 18.1 %gather_fusion.1 = bf16[6144,128]{1,0:T(8,128)(2,1)S(1)} fusion(bf16[3072,128]{1,0:T(8,128)(2,1)S(1)} %pad_maximum_fusion.3, s32[6144]{0:T(1024)S(1)} %broadcast_clamp_fusion), kind=kCustom, calls=%fused_computation.1 | custom fusion | bytes 3170304 | tf_op jit(solution)/shard_map/gather | solution.py:131
  170.9 33.9 %scatter_custom_fusion = f32[3072,128]{1,0:T(8,128)S(1)} fusion(s32[6144]{0:T(1024)} %reshape.1088, f32[6144,128]{1,0:T(8,128)} %bitcast.330, f32[]{:T(128)} %constant.163.clone.1), kind=kCustom, calls=%fused_computation.119 | custom fusion | flops 786432 | bytes 1573376 | tf_op jit(solution)/shard_map/scatter-add | solution.py:140
  205.7 6.4 %all-to-all-start.1 = ((f32[32,32,128]{2,1,0:T(8,128)}), f32[32,32,128]{2,1,0:T(8,128)S(1)}, u32[]{:S(2)}, u32[]{:S(2)}) async-start(f32[32,32,128]{2,1,0:T(8,128)} %bitcast.52), calls=%async_computation.1 | async-start | bytes 1048576 | tf_op jit(solution)/shard_map/all_to_all | solution.py:144
  213.5 9.4 %all_gather.6 = bf16[384,4,128]{2,1,0:T(4,128)(2,1)S(1)} all-gather(bf16[96,4,128]{2,1,0:T(4,128)(2,1)S(1)} %all-to-all-done.2), channel_id=1, replica_groups=mesh['dom'=8,'dir'=4] {'dir'}, dimensions={0}, use_global_device_ids=true | all-gather | bytes 491520 | tf_op jit(solution)/shard_map/all_gather | solution.py:231
  222.9 6.9 %fusion.84 = s32[384]{0:T(512)S(1)} fusion(bf16[384,4,128]{2,1,0:T(4,128)(2,1)S(1)} %all_gather.6), kind=kLoop, calls=%fused_computation.194 | loop fusion | flops 384 | bytes 2304 | tf_op jit(solution)/shard_map/convert_element_type | solution.py:164
  230.6 7.3 %scatter_custom_fusion.1 = f32[2049,128]{1,0:T(8,128)S(1)} fusion(s32[1024]{0:T(1024)} %reshape.1096, f32[1024,128]{1,0:T(8,128)} %bitcast.329, f32[]{:T(128)} %constant.163.clone.1), kind=kCustom, calls=%fused_computation.121 | custom fusion | flops 131072 | bytes 1049600 | tf_op jit(solution)/shard_map/scatter-add | solution.py:151
  237.9 2.3 slice_add_fusion
  240.2 183.6 %while.13 = (s32[]{:T(128)}, f32[16,4,64,128]{3,0,2,1:T(8,128)S(1)}, f32[16,4,64,128]{3,0,2,1:T(8,128)}, s32[3,128]{1,0:T(4,128)S(1)}, bf16[3,128,3,128]{3,1,2,0...) while((s32[]{:T(128)}, ...), condition=%wide.region_6.7_spmd.clone, body=%wide.region_5.6_spmd.clone.sunk | while | flops 2447904768 | bytes 113871504 | solution.py:195
  263.4 2.6 multiply_divide_fusion.15
  269.8 2.6 multiply_divide_fusion.16
  274.4 2.6 multiply_divide_fusion.17
  281.3 7.0 %fusion.152 = bf16[128,4,64,128]{3,2,1,0:T(8,128)(2,1)} fusion(f32[128,4,128]{2,1,0:T(4,128)S(1)} %get-tuple-element.274, f32[128,64,128]{2,1,0:T(8,128)S(1)} %bitcast.320, bf16[3,128,128,128]{3,2,1,0:T(8,128)(2,1)} %get-tuple-element.314, s32[]{:T(128)S(6)} %copy.85), kind=kOutput, calls=%fused_computation.21.clone.1 | convolution fusion | flops 1086324736 | bytes 17039364 | tf_op jit(solution)/shard_map/while/body/eval_jaxpr/gcqb,gbn->gcqn/dot_general | solution.py:174
  288.2 8.2 %select_add_fusion.4 = f32[16,4,64,128]{3,0,2,1:T(8,128)S(1)} fusion(f32[16,4,64,128]{3,0,2,1:T(8,128)S(1)} %get-tuple-element.300, bf16[128,4,64,128]{3,2,1,0:T(8,128)(2,1)} %fusion.152, pred[]{:T(512)S(6)} %compare.55, s32[128]{0:T(128)S(1)} %fusion.153), kind=kOutput, calls=%fused_computation.27.clone.1 | convolution fusion | flops 135268352 | bytes 12583425 | tf_op jit(solution)/shard_map/while/body/eval_jaxpr/lg,gcqn->lcqn/dot_general | solution.py:181
  296.9 4.8 %fusion.154 = bf16[128,4,64,128]{3,2,1,0:T(8,128)(2,1)S(1)} fusion(f32[128,4,128]{2,1,0:T(4,128)S(1)} %get-tuple-element.289, f32[128,64,128]{2,1,0:T(8,128)S(1)} %neg.19, bf16[3,128,128,128]{3,2,1,0:T(8,128)(2,1)} %get-tuple-element.314, s32[]{:T(128)S(6)} %copy.85), kind=kOutput, calls=%fused_computation.20.clone.1 | convolution fusion | flops 1086324736 | bytes 17039364 | tf_op jit(solution)/shard_map/while/body/eval_jaxpr/gcqb,gbn->gcqn/dot_general | solution.py:177
  301.7 6.0 %select_add_fusion.5 = f32[16,4,64,128]{3,0,2,1:T(8,128)} fusion(f32[16,4,64,128]{3,0,2,1:T(8,128)} %get-tuple-element.301, bf16[128,4,64,128]{3,2,1,0:T(8,128)(2,1)S(1)} %fusion.154, pred[]{:T(512)S(6)} %compare.55, s32[128]{0:T(128)S(1)} %fusion.153), kind=kOutput, calls=%fused_computation.26.clone.1 | convolution fusion | flops 135268352 | bytes 12583425 | tf_op jit(solution)/shard_map/while/body/eval_jaxpr/lg,gcqn->lcqn/dot_general | solution.py:184
  319.7 2.6 multiply_divide_fusion.15
  326.1 2.6 multiply_divide_fusion.16
  330.8 2.6 multiply_divide_fusion.17
  337.6 7.0 %fusion.152 = bf16[128,4,64,128]{3,2,1,0:T(8,128)(2,1)} fusion(f32[128,4,128]{2,1,0:T(4,128)S(1)} %get-tuple-element.274, f32[128,64,128]{2,1,0:T(8,128)S(1)} %bitcast.320, bf16[3,128,128,128]{3,2,1,0:T(8,128)(2,1)} %get-tuple-element.314, s32[]{:T(128)S(6)} %copy.85), kind=kOutput, calls=%fused_computation.21.clone.1 | convolution fusion | flops 1086324736 | bytes 17039364 | tf_op jit(solution)/shard_map/while/body/eval_jaxpr/gcqb,gbn->gcqn/dot_general | solution.py:174
  344.6 8.2 %select_add_fusion.4 = f32[16,4,64,128]{3,0,2,1:T(8,128)S(1)} fusion(f32[16,4,64,128]{3,0,2,1:T(8,128)S(1)} %get-tuple-element.300, bf16[128,4,64,128]{3,2,1,0:T(8,128)(2,1)} %fusion.152, pred[]{:T(512)S(6)} %compare.55, s32[128]{0:T(128)S(1)} %fusion.153), kind=kOutput, calls=%fused_computation.27.clone.1 | convolution fusion | flops 135268352 | bytes 12583425 | tf_op jit(solution)/shard_map/while/body/eval_jaxpr/lg,gcqn->lcqn/dot_general | solution.py:181
  353.2 4.8 %fusion.154 = bf16[128,4,64,128]{3,2,1,0:T(8,128)(2,1)S(1)} fusion(f32[128,4,128]{2,1,0:T(4,128)S(1)} %get-tuple-element.289, f32[128,64,128]{2,1,0:T(8,128)S(1)} %neg.19, bf16[3,128,128,128]{3,2,1,0:T(8,128)(2,1)} %get-tuple-element.314, s32[]{:T(128)S(6)} %copy.85), kind=kOutput, calls=%fused_computation.20.clone.1 | convolution fusion | flops 1086324736 | bytes 17039364 | tf_op jit(solution)/shard_map/while/body/eval_jaxpr/gcqb,gbn->gcqn/dot_general | solution.py:177
  358.1 7.6 %select_add_fusion.5 = f32[16,4,64,128]{3,0,2,1:T(8,128)} fusion(f32[16,4,64,128]{3,0,2,1:T(8,128)} %get-tuple-element.301, bf16[128,4,64,128]{3,2,1,0:T(8,128)(2,1)S(1)} %fusion.154, pred[]{:T(512)S(6)} %compare.55, s32[128]{0:T(128)S(1)} %fusion.153), kind=kOutput, calls=%fused_computation.26.clone.1 | convolution fusion | flops 135268352 | bytes 12583425 | tf_op jit(solution)/shard_map/while/body/eval_jaxpr/lg,gcqn->lcqn/dot_general | solution.py:184
  377.6 2.6 multiply_divide_fusion.15
  384.0 2.6 multiply_divide_fusion.16
  388.7 2.6 multiply_divide_fusion.17
  395.5 7.0 %fusion.152 = bf16[128,4,64,128]{3,2,1,0:T(8,128)(2,1)} fusion(f32[128,4,128]{2,1,0:T(4,128)S(1)} %get-tuple-element.274, f32[128,64,128]{2,1,0:T(8,128)S(1)} %bitcast.320, bf16[3,128,128,128]{3,2,1,0:T(8,128)(2,1)} %get-tuple-element.314, s32[]{:T(128)S(6)} %copy.85), kind=kOutput, calls=%fused_computation.21.clone.1 | convolution fusion | flops 1086324736 | bytes 17039364 | tf_op jit(solution)/shard_map/while/body/eval_jaxpr/gcqb,gbn->gcqn/dot_general | solution.py:174
  402.5 8.2 %select_add_fusion.4 = f32[16,4,64,128]{3,0,2,1:T(8,128)S(1)} fusion(f32[16,4,64,128]{3,0,2,1:T(8,128)S(1)} %get-tuple-element.300, bf16[128,4,64,128]{3,2,1,0:T(8,128)(2,1)} %fusion.152, pred[]{:T(512)S(6)} %compare.55, s32[128]{0:T(128)S(1)} %fusion.153), kind=kOutput, calls=%fused_computation.27.clone.1 | convolution fusion | flops 135268352 | bytes 12583425 | tf_op jit(solution)/shard_map/while/body/eval_jaxpr/lg,gcqn->lcqn/dot_general | solution.py:181
  411.2 4.8 %fusion.154 = bf16[128,4,64,128]{3,2,1,0:T(8,128)(2,1)S(1)} fusion(f32[128,4,128]{2,1,0:T(4,128)S(1)} %get-tuple-element.289, f32[128,64,128]{2,1,0:T(8,128)S(1)} %neg.19, bf16[3,128,128,128]{3,2,1,0:T(8,128)(2,1)} %get-tuple-element.314, s32[]{:T(128)S(6)} %copy.85), kind=kOutput, calls=%fused_computation.20.clone.1 | convolution fusion | flops 1086324736 | bytes 17039364 | tf_op jit(solution)/shard_map/while/body/eval_jaxpr/gcqb,gbn->gcqn/dot_general | solution.py:177
  416.0 7.6 %select_add_fusion.5 = f32[16,4,64,128]{3,0,2,1:T(8,128)} fusion(f32[16,4,64,128]{3,0,2,1:T(8,128)} %get-tuple-element.301, bf16[128,4,64,128]{3,2,1,0:T(8,128)(2,1)S(1)} %fusion.154, pred[]{:T(512)S(6)} %compare.55, s32[128]{0:T(128)S(1)} %fusion.153), kind=kOutput, calls=%fused_computation.26.clone.1 | convolution fusion | flops 135268352 | bytes 12583425 | tf_op jit(solution)/shard_map/while/body/eval_jaxpr/lg,gcqn->lcqn/dot_general | solution.py:184
  423.8 2.1 fusion.35
  426.0 3.8 convolution_bitcast_fusion
  429.8 3.8 convolution_bitcast_fusion.2
  433.7 3.8 fusion.33
  437.5 4.1 fusion.31
  (250 shorter events, 61.3 us)
Async XLA Ops:
  7.2 233.1 %all-gather.2.cloned.1.call-start = ((), (), s32[]{:S(2)}) async-start(), calls=%async_computation.3 | async-start | bytes 15728640 | tf_op jit(solution)/shard_map/all_gather | solution.py:230
  18.4 10.9 %collective-permute-start = (bf16[12,128,128]{2,1,0:T(8,128)(2,1)S(1)}, bf16[12,128,128]{2,1,0:T(8,128)(2,1)S(1)}, u32[]{:S(2)}, u32[]{:S(2)}) collective-permute-start(bf16[12,128,128]{2,1,0:T(8,128)(2,1)S(1)} %get-tuple-element.127), channel_id=1, source_target_pairs={{0,4},{4,0},{8,12},{12,8},{16,20},{20,16},{24,28},{28,24},{1,5},{5... | collective-permute-start | bytes 1179656 | tf_op jit(solution)/shard_map/ppermute | solution.py:28
  20.5 25.6 %collective-permute-start.1 = (bf16[12,128,128]{2,1,0:T(8,128)(2,1)S(1)}, bf16[12,128,128]{2,1,0:T(8,128)(2,1)S(1)}, u32[]{:S(2)}, u32[]{:S(2)}) collective-permute-start(bf16[12,128,128]{2,1,0:T(8,128)(2,1)S(1)} %get-tuple-element.126), channel_id=1, source_target_pairs={{0,8},{4,12},{8,0},{12,4},{16,24},{20,28},{24,16},{28,20},{1,9},{5... | collective-permute-start | bytes 1179656 | tf_op jit(solution)/shard_map/ppermute | solution.py:28
  21.8 32.2 %collective-permute-start.2 = (bf16[12,128,128]{2,1,0:T(8,128)(2,1)S(1)}, bf16[12,128,128]{2,1,0:T(8,128)(2,1)S(1)}, u32[]{:S(2)}, u32[]{:S(2)}) collective-permute-start(bf16[12,128,128]{2,1,0:T(8,128)(2,1)S(1)} %get-tuple-element.125), channel_id=1, source_target_pairs={{0,12},{4,8},{8,4},{12,0},{16,28},{20,24},{24,20},{28,16},{1,13},{... | collective-permute-start | bytes 1179656 | tf_op jit(solution)/shard_map/ppermute | solution.py:28
  21.8 32.3 %collective-permute-start.3 = (bf16[12,128,128]{2,1,0:T(8,128)(2,1)S(1)}, bf16[12,128,128]{2,1,0:T(8,128)(2,1)S(1)}, u32[]{:S(2)}, u32[]{:S(2)}) collective-permute-start(bf16[12,128,128]{2,1,0:T(8,128)(2,1)S(1)} %get-tuple-element.124), channel_id=1, source_target_pairs={{0,16},{4,20},{8,24},{12,28},{16,0},{20,4},{24,8},{28,12},{1,17},{... | collective-permute-start | bytes 1179656 | tf_op jit(solution)/shard_map/ppermute | solution.py:28
  24.2 30.4 %collective-permute-start.4 = (bf16[12,128,128]{2,1,0:T(8,128)(2,1)S(1)}, bf16[12,128,128]{2,1,0:T(8,128)(2,1)S(1)}, u32[]{:S(2)}, u32[]{:S(2)}) collective-permute-start(bf16[12,128,128]{2,1,0:T(8,128)(2,1)S(1)} %get-tuple-element.123), channel_id=1, source_target_pairs={{0,20},{4,16},{8,28},{12,24},{16,4},{20,0},{24,12},{28,8},{1,21},{... | collective-permute-start | bytes 1179656 | tf_op jit(solution)/shard_map/ppermute | solution.py:28
  29.3 36.7 %collective-permute-start.5 = (bf16[12,128,128]{2,1,0:T(8,128)(2,1)S(1)}, bf16[12,128,128]{2,1,0:T(8,128)(2,1)S(1)}, u32[]{:S(2)}, u32[]{:S(2)}) collective-permute-start(bf16[12,128,128]{2,1,0:T(8,128)(2,1)S(1)} %get-tuple-element.122), channel_id=1, source_target_pairs={{0,24},{4,28},{8,16},{12,20},{16,8},{20,12},{24,0},{28,4},{1,25},{... | collective-permute-start | bytes 1179656 | tf_op jit(solution)/shard_map/ppermute | solution.py:28
  46.1 28.2 %collective-permute-start.6 = (bf16[12,128,128]{2,1,0:T(8,128)(2,1)S(1)}, bf16[12,128,128]{2,1,0:T(8,128)(2,1)S(1)}, u32[]{:S(2)}, u32[]{:S(2)}) collective-permute-start(bf16[12,128,128]{2,1,0:T(8,128)(2,1)S(1)} %get-tuple-element.121), channel_id=1, source_target_pairs={{0,28},{4,24},{8,20},{12,16},{16,12},{20,8},{24,4},{28,0},{1,29},{... | collective-permute-start | bytes 1179656 | tf_op jit(solution)/shard_map/ppermute | solution.py:28
  77.0 44.9 %copy-start.12 = (s32[6,1024]{1,0:T(8,128)S(1)}, s32[6,1024]{1,0:T(8,128)}, u32[]{:S(2)}) copy-start(s32[6,1024]{1,0:T(8,128)} %param.15) | copy-start | bytes 73732
  77.0 44.9 %copy-start.57 = (s32[32]{0:T(128)S(1)}, s32[32]{0:T(128)}, u32[]{:S(2)}) copy-start(s32[32]{0:T(128)} %param.22) | copy-start | bytes 388
  77.0 44.9 %copy-start.16 = (bf16[32,3,128]{2,0,1:T(8,128)(2,1)S(1)}, bf16[32,3,128]{2,0,1:T(8,128)(2,1)}, u32[]{:S(2)}) copy-start(bf16[32,3,128]{2,0,1:T(8,128)(2,1)} %param.19) | copy-start | bytes 73732
  77.0 48.4 %copy-start.15 = (f32[3,4]{1,0:T(4,128)S(1)}, f32[3,4]{1,0:T(4,128)}, u32[]{:S(2)}) copy-start(f32[3,4]{1,0:T(4,128)} %param.23) | copy-start | bytes 148
  77.0 49.0 %copy-start.11 = (f32[36,1024]{1,0:T(8,128)S(1)}, f32[36,1024]{1,0:T(8,128)}, u32[]{:S(2)}) copy-start(f32[36,1024]{1,0:T(8,128)} %param.16) | copy-start | bytes 442372
  78.1 49.2 %copy-start.14 = (s32[32,32]{1,0:T(8,128)S(1)}, s32[32,32]{1,0:T(8,128)}, u32[]{:S(2)}) copy-start(s32[32,32]{1,0:T(8,128)} %param.14) | copy-start | bytes 12292
  82.4 54.9 %all-to-all-start = ((bf16[32,32,128]{2,1,0:T(8,128)(2,1)}), bf16[32,32,128]{2,1,0:T(8,128)(2,1)S(1)}, u32[]{:S(2)}, u32[]{:S(2)}) async-start(bf16[32,32,128]{2,1,0:T(8,128)(2,1)} %bitcast.2), calls=%async_computation | async-start | bytes 524288 | tf_op jit(solution)/shard_map/all_to_all | solution.py:129
  122.2 7.9 %copy-start.49 = (f32[3,64]{1,0:T(4,128)}, f32[3,64]{1,0:T(4,128)S(1)}, u32[]{:S(2)}) copy-start(f32[3,64]{1,0:T(4,128)S(1)} %get-tuple-element.184) | copy-start | bytes 2308
  137.3 68.4 %all-to-all-start.2 = ((bf16[96,4,128]{2,1,0:T(4,128)(2,1)}), bf16[96,4,128]{2,1,0:T(4,128)(2,1)S(1)}, u32[]{:S(2)}, u32[]{:S(2)}) async-start(bf16[96,4,128]{2,1,0:T(4,128)(2,1)} %gather_fusion.2), calls=%async_computation.2 | async-start | bytes 196608 | tf_op jit(solution)/shard_map/all_to_all | solution.py:227
  143.1 18.3 %copy-start.24 = (f32[1,1024]{1,0:T(1,128)S(1)}, f32[1,1024]{1,0:T(1,128)}, u32[]{:S(2)}) copy-start(f32[1,1024]{1,0:T(1,128)} %get-tuple-element.161) | copy-start | bytes 12292
  143.1 18.3 %copy-start.25 = (f32[1,1024]{1,0:T(1,128)S(1)}, f32[1,1024]{1,0:T(1,128)}, u32[]{:S(2)}) copy-start(f32[1,1024]{1,0:T(1,128)} %get-tuple-element.162) | copy-start | bytes 12292
  143.1 18.3 %copy-start.26 = (f32[1,1024]{1,0:T(1,128)S(1)}, f32[1,1024]{1,0:T(1,128)}, u32[]{:S(2)}) copy-start(f32[1,1024]{1,0:T(1,128)} %get-tuple-element.163) | copy-start | bytes 12292
  143.1 18.3 %copy-start.27 = (f32[1,1024]{1,0:T(1,128)S(1)}, f32[1,1024]{1,0:T(1,128)}, u32[]{:S(2)}) copy-start(f32[1,1024]{1,0:T(1,128)} %get-tuple-element.164) | copy-start | bytes 12292
  143.1 18.3 %copy-start.28 = (f32[1,1024]{1,0:T(1,128)S(1)}, f32[1,1024]{1,0:T(1,128)}, u32[]{:S(2)}) copy-start(f32[1,1024]{1,0:T(1,128)} %get-tuple-element.165) | copy-start | bytes 12292
  143.1 18.3 %copy-start.29 = (f32[1,1024]{1,0:T(1,128)S(1)}, f32[1,1024]{1,0:T(1,128)}, u32[]{:S(2)}) copy-start(f32[1,1024]{1,0:T(1,128)} %get-tuple-element.166) | copy-start | bytes 12292
  143.1 19.5 %copy-start.18 = (f32[1,1024]{1,0:T(1,128)S(1)}, f32[1,1024]{1,0:T(1,128)}, u32[]{:S(2)}) copy-start(f32[1,1024]{1,0:T(1,128)} %get-tuple-element.155) | copy-start | bytes 12292
  143.2 19.5 %copy-start.19 = (f32[1,1024]{1,0:T(1,128)S(1)}, f32[1,1024]{1,0:T(1,128)}, u32[]{:S(2)}) copy-start(f32[1,1024]{1,0:T(1,128)} %get-tuple-element.156) | copy-start | bytes 12292
  143.2 19.5 %copy-start.20 = (f32[1,1024]{1,0:T(1,128)S(1)}, f32[1,1024]{1,0:T(1,128)}, u32[]{:S(2)}) copy-start(f32[1,1024]{1,0:T(1,128)} %get-tuple-element.157) | copy-start | bytes 12292
  143.2 19.5 %copy-start.21 = (f32[1,1024]{1,0:T(1,128)S(1)}, f32[1,1024]{1,0:T(1,128)}, u32[]{:S(2)}) copy-start(f32[1,1024]{1,0:T(1,128)} %get-tuple-element.158) | copy-start | bytes 12292
  143.2 19.5 %copy-start.22 = (f32[1,1024]{1,0:T(1,128)S(1)}, f32[1,1024]{1,0:T(1,128)}, u32[]{:S(2)}) copy-start(f32[1,1024]{1,0:T(1,128)} %get-tuple-element.159) | copy-start | bytes 12292
  143.2 19.5 %copy-start.23 = (f32[1,1024]{1,0:T(1,128)S(1)}, f32[1,1024]{1,0:T(1,128)}, u32[]{:S(2)}) copy-start(f32[1,1024]{1,0:T(1,128)} %get-tuple-element.160) | copy-start | bytes 12292
  161.4 3.9 copy-start.40
  161.4 3.9 copy-start.41
  161.4 3.9 copy-start.42
  161.4 3.9 copy-start.43
  161.4 3.9 copy-start.44
  167.9 44.2 %copy-start.51 = (f32[4]{0:T(128)S(1)}, f32[4]{0:T(128)}, u32[]{:S(2)}) copy-start(f32[4]{0:T(128)} %get-tuple-element.177) | copy-start | bytes 52
  167.9 44.2 %copy-start.52 = (f32[4]{0:T(128)S(1)}, f32[4]{0:T(128)}, u32[]{:S(2)}) copy-start(f32[4]{0:T(128)} %get-tuple-element.178) | copy-start | bytes 52
  167.9 44.2 %copy-start.53 = (f32[4]{0:T(128)S(1)}, f32[4]{0:T(128)}, u32[]{:S(2)}) copy-start(f32[4]{0:T(128)} %get-tuple-element.179) | copy-start | bytes 52
  167.9 44.2 %copy-start.54 = (f32[64]{0:T(128)S(1)}, f32[64]{0:T(128)}, u32[]{:S(2)}) copy-start(f32[64]{0:T(128)} %get-tuple-element.180) | copy-start | bytes 772
  167.9 44.2 %copy-start.55 = (f32[64]{0:T(128)S(1)}, f32[64]{0:T(128)}, u32[]{:S(2)}) copy-start(f32[64]{0:T(128)} %get-tuple-element.181) | copy-start | bytes 772
  167.9 44.2 %copy-start.56 = (f32[64]{0:T(128)S(1)}, f32[64]{0:T(128)}, u32[]{:S(2)}) copy-start(f32[64]{0:T(128)} %get-tuple-element.182) | copy-start | bytes 772
  168.0 44.3 %copy-start.50 = (f32[3,64]{1,0:T(4,128)S(1)}, f32[3,64]{1,0:T(4,128)}, u32[]{:S(2)}) copy-start(f32[3,64]{1,0:T(4,128)} %copy-done.49) | copy-start | bytes 2308
  204.8 7.8 %copy-start.3 = (f32[3072,128]{1,0:T(8,128)}, f32[3072,128]{1,0:T(8,128)S(1)}, u32[]{:S(2)}) copy-start(f32[3072,128]{1,0:T(8,128)S(1)} %scatter_custom_fusion) | copy-start | bytes 4718596
  205.7 24.1 %all-to-all-start.1 = ((f32[32,32,128]{2,1,0:T(8,128)}), f32[32,32,128]{2,1,0:T(8,128)S(1)}, u32[]{:S(2)}, u32[]{:S(2)}) async-start(f32[32,32,128]{2,1,0:T(8,128)} %bitcast.52), calls=%async_computation.1 | async-start | bytes 1048576 | tf_op jit(solution)/shard_map/all_to_all | solution.py:144
  213.5 26.7 %copy-start.2 = (f32[16,4,64,128]{3,0,2,1:T(8,128)S(1)}, f32[16,4,64,128]{3,0,2,1:T(8,128)}, u32[]{:S(2)}) copy-start(f32[16,4,64,128]{3,0,2,1:T(8,128)} %custom-call) | copy-start | bytes 6291460
  288.2 8.2 %copy-start.1 = (f32[128,4,4,4,128]{4,3,2,1,0:T(4,128)S(1)}, f32[128,4,4,4,128]{4,3,2,1,0:T(4,128)}, u32[]{:S(2)}) copy-start(f32[128,4,4,4,128]{4,3,2,1,0:T(4,128)} %copy-done) | copy-start | bytes 12582916 | tf_op jit(solution)/shard_map/while
  344.6 8.2 %copy-start.1 = (f32[128,4,4,4,128]{4,3,2,1,0:T(4,128)S(1)}, f32[128,4,4,4,128]{4,3,2,1,0:T(4,128)}, u32[]{:S(2)}) copy-start(f32[128,4,4,4,128]{4,3,2,1,0:T(4,128)} %copy-done) | copy-start | bytes 12582916 | tf_op jit(solution)/shard_map/while
  402.5 8.2 %copy-start.1 = (f32[128,4,4,4,128]{4,3,2,1,0:T(4,128)S(1)}, f32[128,4,4,4,128]{4,3,2,1,0:T(4,128)}, u32[]{:S(2)}) copy-start(f32[128,4,4,4,128]{4,3,2,1,0:T(4,128)} %copy-done) | copy-start | bytes 12582916 | tf_op jit(solution)/shard_map/while
  426.0 7.7 %copy-start.6 = (f32[8,64,64]{1,0,2:T(8,128)S(1)}, f32[8,64,64]{1,0,2:T(8,128)}, u32[]{:S(2)}) copy-start(f32[8,64,64]{1,0,2:T(8,128)} %copy.37) | copy-start | bytes 393220
  (25 other events, 71.8 us)
Sparse Core Ops, SparseCore 0:
  77.2 103.9 all-gather.1
